TPU v7x, 32 devices: a whole 2x2x4 slice. The times are simulated.
32 devices in a mesh: feat: 4 (over y, core), dom: 8 (over z, x).
Axes of the slice: x: 2, y: 2, z: 4, core: 2. Of those that a mesh axis runs over, the one named last changes fastest.
Arguments:
- features: bfloat16 [32768, 128], P('dom'), may hold values from -6 to 6
- w_input: bfloat16 [128, 256], P(None, 'feat'), may hold values from -0.5 to 0.5
- layer_weights: bfloat16 [4, 256, 256], replicated, may hold values from -0.375 to 0.375
- history: bfloat16 [4, 32768, 256], P(None, 'dom', 'feat'), may hold values from 0 to 2
- tile_values: bfloat16 [256, 6, 128, 128], P('dom'), may hold values from -0.21875 to 0.21875
- tile_columns: int32 [256, 6], P('dom'), may hold values from 0 to 63, as said below
- send_rows: int32 [8, 8, 512], P('dom'), may hold values from 0 to 4095
- send_counts: int32 [8, 8], P('dom'), may hold values from 0 to 512, as said below
Outputs:
- pushed: bfloat16 [4, 32768, 256], P(None, 'dom', 'feat')
- final_rows: bfloat16 [32768, 256], P('dom', 'feat')
Inputs may be any that keep to these rules, and one draw needn't show every extreme that they name: `tile_columns`: per row of tiles the first 2 entries lie below 4096 / 128 (own rows), the others at or above it (halo slots); every halo column tile of every partition is named somewhere. `send_counts`: A partition sends nothing to itself; in every draw some destination receives exactly 512 rows from every other partition.
All inputs are finite; a program needn't handle non-finite values.
Results may differ from a plain program's by a relative error of at most 0.0052.
Values may be sent and summed in bfloat16 or wider, within the bound.
A program may use at most 128 MiB of HBM per device.

v0:
```python
import math
import jax
import jax.numpy as jnp
from jax import lax
from jax.sharding import PartitionSpec as P

LAYERS = 4
ALPHA = 0.1
LAMBDA_DECAY = 0.5


def propagate(own_rows, halo_rows, values, columns, tile_size):
    slice_width = own_rows.shape[1]
    combined = jnp.concatenate([own_rows, halo_rows], axis=0)
    tile_count = combined.shape[0] // tile_size
    flat_tiles = combined.reshape(tile_count, tile_size * slice_width)
    row_tiles, per_row = columns.shape
    selector = (
        columns.reshape(row_tiles * per_row, 1) == jnp.arange(tile_count, dtype=jnp.int32)[None, :]
    ).astype(jnp.bfloat16)
    picked = jnp.dot(selector, flat_tiles, preferred_element_type=jnp.float32).astype(jnp.bfloat16)
    picked = picked.reshape(row_tiles, per_row, tile_size, slice_width)
    summed = jnp.einsum("rkab,rkbf->raf", values, picked, preferred_element_type=jnp.float32)
    return summed.reshape(own_rows.shape[0], slice_width)


def on_device(
    features, w_input, layer_weights, history, tile_values, tile_columns, send_rows, send_counts
):
    initial = jnp.maximum(
        jnp.dot(features, w_input, preferred_element_type=jnp.float32), 0.0
    ).astype(jnp.bfloat16)
    nodes_local, slice_width = initial.shape
    peer_count = send_rows.shape[1]
    slot_count = send_rows.shape[2]
    tile_size = tile_values.shape[-1]
    targets = send_rows[0]
    live_slots = (jnp.arange(slot_count)[None, :] < send_counts[0][:, None])[:, :, None]
    zero_value = jnp.zeros((), jnp.bfloat16)
    halo_list = [
        lax.all_to_all(
            jnp.where(live_slots, history[level][targets], zero_value),
            "dom",
            split_axis=0,
            concat_axis=0,
            tiled=True,
        ).reshape(peer_count * slot_count, slice_width)
        for level in range(LAYERS)
    ]
    pushed = []
    current = initial
    for layer_index in range(LAYERS):
        beta_layer = math.log(LAMBDA_DECAY / (layer_index + 1) + 1.0)
        weight = layer_weights[layer_index]
        aggregated = propagate(
            current, halo_list[layer_index], tile_values, tile_columns, tile_size
        )
        blended = ((1.0 - ALPHA) * aggregated + ALPHA * initial.astype(jnp.float32)).astype(
            jnp.bfloat16
        )
        blended = lax.optimization_barrier(blended)
        pushed.append(current)
        feat_index = lax.axis_index("feat")
        weight_cols = lax.dynamic_slice_in_dim(weight, feat_index * slice_width, slice_width, 1)
        product = jnp.dot(
            lax.all_gather(blended, "feat", axis=1, tiled=True),
            weight_cols,
            preferred_element_type=jnp.float32,
        )
        fresh = jnp.maximum(
            (1.0 - beta_layer) * blended.astype(jnp.float32) + beta_layer * product, 0.0
        )
        current = fresh.astype(jnp.bfloat16)
    return (jnp.stack(pushed), current)


def solution(mesh):
    placed = (
        P("dom", None),
        P(None, "feat"),
        P(),
        P(None, "dom", "feat"),
        P("dom", None, None, None),
        P("dom", None),
        P("dom", None, None),
        P("dom", None),
    )
    return jax.shard_map(
        on_device,
        mesh=mesh,
        in_specs=placed,
        out_specs=(P(None, "dom", "feat"), P("dom", "feat")),
        check_vma=False,
    )
```

profile of v0, /device:TPU:0, one launch (start us, length us, event | category | flops | bytes accessed | tf_op | source)
XLA Modules:
  0.0 316.9 jit_solution(15745469783871784883)
XLA Ops:
  7.2 2.8 fusion.42
  10.5 15.0 %gather_fusion = bf16[4096,64]{1,0:T(8,128)(2,1)} fusion(bf16[4096,64]{1,0:T(8,128)(2,1)S(1)} %bitcast.113, s32[4096]{0:T(1024)S(1)} %broadcast_clamp_fusion), kind=kCustom, calls=%fused_computation | custom fusion | bytes 1064960 | tf_op jit(solution)/shard_map/gather | solution.py:42
  25.5 1.5 copy.49
  27.6 15.0 %gather_fusion.1 = bf16[4096,64]{1,0:T(8,128)(2,1)} fusion(bf16[4096,64]{1,0:T(8,128)(2,1)S(1)} %bitcast.115, s32[4096]{0:T(1024)S(1)} %broadcast_clamp_fusion), kind=kCustom, calls=%fused_computation.1 | custom fusion | bytes 1064960 | tf_op jit(solution)/shard_map/gather | solution.py:42
  42.6 1.5 copy.55
  44.2 1.5 copy.82
  45.7 15.0 %gather_fusion.2 = bf16[4096,64]{1,0:T(8,128)(2,1)} fusion(bf16[4096,64]{1,0:T(8,128)(2,1)S(1)} %bitcast.116, s32[4096]{0:T(1024)S(1)} %broadcast_clamp_fusion), kind=kCustom, calls=%fused_computation.2 | custom fusion | bytes 1064960 | tf_op jit(solution)/shard_map/gather | solution.py:42
  60.7 2.4 copy.61
  63.1 1.5 copy.83
  64.6 15.0 %gather_fusion.3 = bf16[4096,64]{1,0:T(8,128)(2,1)} fusion(bf16[4096,64]{1,0:T(8,128)(2,1)S(1)} %bitcast.114, s32[4096]{0:T(1024)S(1)} %broadcast_clamp_fusion), kind=kCustom, calls=%fused_computation.3 | custom fusion | bytes 1064960 | tf_op jit(solution)/shard_map/gather | solution.py:42
  79.7 1.5 copy.67
  81.3 2.4 broadcast_select_fusion
  83.7 7.3 %all-to-all-start = ((bf16[8,512,64]{1,2,0:T(8,128)(2,1)}), bf16[8,512,64]{1,2,0:T(8,128)(2,1)S(1)}, u32[]{:S(2)}, u32[]{:S(2)}) async-start(bf16[8,512,64]{1,2,0:T(8,128)(2,1)} %get-tuple-element.13), calls=%async_computation | async-start | bytes 1048576 | tf_op jit(solution)/shard_map/all_to_all | solution.py:41
  91.7 13.7 %all-to-all-done = bf16[8,512,64]{1,2,0:T(8,128)(2,1)S(1)} async-done(((bf16[8,512,64]{1,2,0:T(8,128)(2,1)}), bf16[8,512,64]{1,2,0:T(8,128)(2,1)S(1)}, u32[]{:S(2)}, u32[]{:S(2)}) %all-to-all-start) | async-done | bytes 524320 | tf_op jit(solution)/shard_map/all_to_all | solution.py:41
  105.6 1.8 copy.51
  107.4 3.3 %reshape.114 = bf16[64,8192]{1,0:T(8,128)(2,1)S(1)} reshape(bf16[8192,64]{1,0:T(8,128)(2,1)} %copy.51) | data formatting | bytes 2097152 | tf_op jit(solution)/shard_map/reshape | solution.py:16
  110.7 2.7 convolution_convert_fusion.3
  113.4 9.7 %reshape.115 = bf16[32,6,128,64]{3,2,1,0:T(8,128)(2,1)} reshape(bf16[192,8192]{1,0:T(8,128)(2,1)} %convolution_convert_fusion.3) | data formatting | bytes 6291456 | tf_op jit(solution)/shard_map/reshape | solution.py:22
  123.1 6.8 %fusion.14 = f32[32,8,8,128]{3,2,1,0:T(8,128)S(1)} fusion(bf16[32,6,128,64]{3,2,1,0:T(8,128)(2,1)} %reshape.115, bf16[32,6,128,128]{3,2,1,0:T(8,128)(2,1)} %param.12), kind=kOutput, calls=%fused_computation.32 | convolution fusion | flops 402915328 | bytes 10485760 | tf_op jit(solution)/shard_map/rkab,rkbf->raf/dot_general | solution.py:23
  130.8 3.8 %all-to-all-start.1 = ((bf16[8,512,64]{1,2,0:T(8,128)(2,1)}), bf16[8,512,64]{1,2,0:T(8,128)(2,1)S(1)}, u32[]{:S(2)}, u32[]{:S(2)}) async-start(bf16[8,512,64]{1,2,0:T(8,128)(2,1)} %get-tuple-element.11), calls=%async_computation.1 | async-start | bytes 1048576 | tf_op jit(solution)/shard_map/all_to_all | solution.py:41
  134.9 14.4 %all-to-all-done.1 = bf16[8,512,64]{1,2,0:T(8,128)(2,1)S(1)} async-done(((bf16[8,512,64]{1,2,0:T(8,128)(2,1)}), bf16[8,512,64]{1,2,0:T(8,128)(2,1)S(1)}, u32[]{:S(2)}, u32[]{:S(2)}) %all-to-all-start.1) | async-done | bytes 524320 | tf_op jit(solution)/shard_map/all_to_all | solution.py:41
  149.3 3.3 %all-gather.5.cloned.1.call-done = bf16[4096,256]{0,1:T(8,128)(2,1)} async-done(((bf16[4096,64]{0,1:T(8,128)(2,1)}), bf16[4096,256]{0,1:T(8,128)(2,1)}) %all-gather.5.cloned.1.call-update) | async-done | bytes 2097168 | tf_op jit(solution)/shard_map/all_gather | solution.py:66
  152.6 2.2 fusion.11
  154.9 1.8 copy.57
  156.7 3.3 %reshape.117 = bf16[64,8192]{1,0:T(8,128)(2,1)S(1)} reshape(bf16[8192,64]{1,0:T(8,128)(2,1)} %copy.57) | data formatting | bytes 2097152 | tf_op jit(solution)/shard_map/reshape | solution.py:16
  160.0 2.7 convolution_convert_fusion.2
  162.7 9.7 %reshape.118 = bf16[32,6,128,64]{3,2,1,0:T(8,128)(2,1)} reshape(bf16[192,8192]{1,0:T(8,128)(2,1)} %convolution_convert_fusion.2) | data formatting | bytes 6291456 | tf_op jit(solution)/shard_map/reshape | solution.py:22
  172.4 6.8 %fusion.16 = f32[32,8,8,128]{3,2,1,0:T(8,128)S(1)} fusion(bf16[32,6,128,64]{3,2,1,0:T(8,128)(2,1)} %reshape.118, bf16[32,6,128,128]{3,2,1,0:T(8,128)(2,1)} %param.12), kind=kOutput, calls=%fused_computation.34 | convolution fusion | flops 402915328 | bytes 10485760 | tf_op jit(solution)/shard_map/rkab,rkbf->raf/dot_general | solution.py:23
  180.2 20.3 %all_to_all.20 = bf16[8,512,64]{1,2,0:T(8,128)(2,1)S(1)} all-to-all(bf16[8,512,64]{1,2,0:T(8,128)(2,1)S(1)} %copy-done.8), channel_id=1, replica_groups=mesh['feat'=4,'dom'=8] {'dom'}, dimensions={0} | all-to-all | bytes 1048576 | tf_op jit(solution)/shard_map/all_to_all | solution.py:41
  200.6 2.2 all-gather.7.cloned.1.call-done
  202.8 2.2 fusion.10
  205.1 1.8 copy.63
  206.9 3.3 %reshape.120 = bf16[64,8192]{1,0:T(8,128)(2,1)S(1)} reshape(bf16[8192,64]{1,0:T(8,128)(2,1)} %copy.63) | data formatting | bytes 2097152 | tf_op jit(solution)/shard_map/reshape | solution.py:16
  210.2 2.7 convolution_convert_fusion.1
  212.9 9.7 %reshape.121 = bf16[32,6,128,64]{3,2,1,0:T(8,128)(2,1)} reshape(bf16[192,8192]{1,0:T(8,128)(2,1)} %convolution_convert_fusion.1) | data formatting | bytes 6291456 | tf_op jit(solution)/shard_map/reshape | solution.py:22
  222.6 6.8 %fusion.18 = f32[32,8,8,128]{3,2,1,0:T(8,128)S(1)} fusion(bf16[32,6,128,64]{3,2,1,0:T(8,128)(2,1)} %reshape.121, bf16[32,6,128,128]{3,2,1,0:T(8,128)(2,1)} %param.12), kind=kOutput, calls=%fused_computation.36 | convolution fusion | flops 402915328 | bytes 10485760 | tf_op jit(solution)/shard_map/rkab,rkbf->raf/dot_general | solution.py:23
  230.4 20.3 %all_to_all.21 = bf16[8,512,64]{1,2,0:T(8,128)(2,1)S(1)} all-to-all(bf16[8,512,64]{1,2,0:T(8,128)(2,1)S(1)} %copy-done.7), channel_id=1, replica_groups=mesh['feat'=4,'dom'=8] {'dom'}, dimensions={0} | all-to-all | bytes 1048576 | tf_op jit(solution)/shard_map/all_to_all | solution.py:41
  250.8 2.2 all-gather.9.cloned.1.call-done
  253.1 2.2 fusion.9
  255.3 1.1 pad_maximum_fusion.4
  256.4 2.7 copy.69
  259.1 4.2 %reshape.123 = bf16[64,8192]{1,0:T(8,128)(2,1)} reshape(bf16[8192,64]{1,0:T(8,128)(2,1)} %copy.69) | data formatting | bytes 2097152 | tf_op jit(solution)/shard_map/reshape | solution.py:16
  263.3 3.9 %convolution_convert_fusion = bf16[192,8192]{1,0:T(8,128)(2,1)} fusion(bf16[64,8192]{1,0:T(8,128)(2,1)} %reshape.123, s32[192]{0:T(256)S(1)} %eq.8), kind=kOutput, calls=%fused_computation.4 | convolution fusion | flops 202911744 | bytes 4195072 | tf_op jit(solution)/shard_map/dot_general | solution.py:21
  267.3 9.7 %reshape.124 = bf16[32,6,128,64]{3,2,1,0:T(8,128)(2,1)} reshape(bf16[192,8192]{1,0:T(8,128)(2,1)} %convolution_convert_fusion) | data formatting | bytes 6291456 | tf_op jit(solution)/shard_map/reshape | solution.py:22
  276.9 6.8 %fusion.20 = f32[32,8,8,128]{3,2,1,0:T(8,128)S(1)} fusion(bf16[32,6,128,64]{3,2,1,0:T(8,128)(2,1)} %reshape.124, bf16[32,6,128,128]{3,2,1,0:T(8,128)(2,1)} %param.12), kind=kOutput, calls=%fused_computation.38 | convolution fusion | flops 402915328 | bytes 10485760 | tf_op jit(solution)/shard_map/rkab,rkbf->raf/dot_general | solution.py:23
  284.7 2.7 pad_maximum_fusion
  287.4 19.9 %all-gather.11.cloned.1.call-done = bf16[4096,256]{0,1:T(8,128)(2,1)} async-done(((bf16[4096,64]{0,1:T(8,128)(2,1)}), bf16[4096,256]{0,1:T(8,128)(2,1)}) %all-gather.11.cloned.1.call-update) | async-done | bytes 2097168 | tf_op jit(solution)/shard_map/all_gather | solution.py:66
  307.4 3.0 fusion.8
  (57 shorter events, 6.4 us)
Async XLA Ops:
  7.2 84.1 %copy-start = (bf16[4096,128]{1,0:T(8,128)(2,1)S(1)}, bf16[4096,128]{1,0:T(8,128)(2,1)}, u32[]{:S(2)}) copy-start(bf16[4096,128]{1,0:T(8,128)(2,1)} %param.8) | copy-start | bytes 3145732
  7.2 3.3 %copy-start.11 = (s32[1,8,512]{2,1,0:T(8,128)S(1)}, s32[1,8,512]{2,1,0:T(8,128)}, u32[]{:S(2)}) copy-start(s32[1,8,512]{2,1,0:T(8,128)} %param.14) | copy-start | bytes 49156
  64.6 16.6 %copy-start.13 = (s32[1,8]{1,0:T(1,128)S(1)}, s32[1,8]{1,0:T(1,128)}, u32[]{:S(2)}) copy-start(s32[1,8]{1,0:T(1,128)} %param.15) | copy-start | bytes 100
  81.3 9.7 %copy-start.12 = (s32[32,6]{0,1:T(8,128)S(1)}, s32[32,6]{0,1:T(8,128)}, u32[]{:S(2)}) copy-start(s32[32,6]{0,1:T(8,128)} %param.13) | copy-start | bytes 2308
  81.3 9.9 %copy-start.10 = (bf16[128,64]{0,1:T(8,128)(2,1)S(1)}, bf16[128,64]{0,1:T(8,128)(2,1)}, u32[]{:S(2)}) copy-start(bf16[128,64]{0,1:T(8,128)(2,1)} %param.9) | copy-start | bytes 49156
  83.7 21.8 %all-to-all-start = ((bf16[8,512,64]{1,2,0:T(8,128)(2,1)}), bf16[8,512,64]{1,2,0:T(8,128)(2,1)S(1)}, u32[]{:S(2)}, u32[]{:S(2)}) async-start(bf16[8,512,64]{1,2,0:T(8,128)(2,1)} %get-tuple-element.13), calls=%async_computation | async-start | bytes 1048576 | tf_op jit(solution)/shard_map/all_to_all | solution.py:41
  91.0 61.6 %all-gather.5.cloned.1.call-start = ((), (), s32[]{:S(2)}) async-start(), calls=%async_computation.4 | async-start | bytes 2621440 | tf_op jit(solution)/shard_map/all_gather | solution.py:66
  129.8 5.0 %copy-start.9 = (bf16[4,256,256]{2,1,0:T(8,128)(2,1)S(1)}, bf16[4,256,256]{2,1,0:T(8,128)(2,1)}, u32[]{:S(2)}) copy-start(bf16[4,256,256]{2,1,0:T(8,128)(2,1)} %param.10) | copy-start | bytes 1572868
  130.8 21.8 %copy-start.2 = (bf16[4096,64]{0,1:T(8,128)(2,1)S(1)}, bf16[4096,64]{0,1:T(8,128)(2,1)}, u32[]{:S(2)}) copy-start(bf16[4096,64]{0,1:T(8,128)(2,1)} %fusion.24) | copy-start | bytes 1572868
  130.8 18.4 %all-to-all-start.1 = ((bf16[8,512,64]{1,2,0:T(8,128)(2,1)}), bf16[8,512,64]{1,2,0:T(8,128)(2,1)S(1)}, u32[]{:S(2)}, u32[]{:S(2)}) async-start(bf16[8,512,64]{1,2,0:T(8,128)(2,1)} %get-tuple-element.11), calls=%async_computation.1 | async-start | bytes 1048576 | tf_op jit(solution)/shard_map/all_to_all | solution.py:41
  134.6 68.2 %all-gather.7.cloned.1.call-start = ((), (), s32[]{:S(2)}) async-start(), calls=%async_computation.5 | async-start | bytes 2621440 | tf_op jit(solution)/shard_map/all_gather | solution.py:66
  179.2 1.1 copy-start.8
  180.1 22.7 %copy-start.5 = (bf16[4096,64]{0,1:T(8,128)(2,1)S(1)}, bf16[4096,64]{0,1:T(8,128)(2,1)}, u32[]{:S(2)}) copy-start(bf16[4096,64]{0,1:T(8,128)(2,1)} %fusion.23) | copy-start | bytes 1572868
  180.1 72.9 %all-gather.9.cloned.1.call-start = ((), (), s32[]{:S(2)}) async-start(), calls=%async_computation.6 | async-start | bytes 2621440 | tf_op jit(solution)/shard_map/all_gather | solution.py:66
  229.4 1.1 copy-start.7
  230.3 22.7 %copy-start.3 = (bf16[4096,64]{0,1:T(8,128)(2,1)S(1)}, bf16[4096,64]{0,1:T(8,128)(2,1)}, u32[]{:S(2)}) copy-start(bf16[4096,64]{0,1:T(8,128)(2,1)} %fusion.22) | copy-start | bytes 1572868
  230.3 77.0 %all-gather.11.cloned.1.call-start = ((), (), s32[]{:S(2)}) async-start(), calls=%async_computation.7 | async-start | bytes 2621440 | tf_op jit(solution)/shard_map/all_gather | solution.py:66
  255.3 3.9 %copy-start.6 = (bf16[4096,64]{0,1:T(8,128)(2,1)}, bf16[4096,64]{0,1:T(8,128)(2,1)S(1)}, u32[]{:S(2)}) copy-start(bf16[4096,64]{0,1:T(8,128)(2,1)S(1)} %fusion.9) | copy-start | bytes 1572868
  284.7 22.7 %copy-start.4 = (bf16[4096,64]{0,1:T(8,128)(2,1)S(1)}, bf16[4096,64]{0,1:T(8,128)(2,1)}, u32[]{:S(2)}) copy-start(bf16[4096,64]{0,1:T(8,128)(2,1)} %fusion.21) | copy-start | bytes 1572868
  284.7 25.7 %copy-start.1 = (bf16[4096,128]{1,0:T(8,128)(2,1)S(1)}, bf16[4096,128]{1,0:T(8,128)(2,1)}, u32[]{:S(2)}) copy-start(bf16[4096,128]{1,0:T(8,128)(2,1)} %param.8) | copy-start | bytes 3145732
Sparse Core Ops, SparseCore 0:
  130.9 21.6 all-gather.4
  180.2 22.5 all-gather.6
  230.5 22.5 all-gather.8
  284.8 22.5 all-gather.10
where the time goes:
time: 319 us; the launch traced here: 317 us
  local copies, waits for them, and re-layouts  135 us (42%)
  waiting for transfers between devices  55.9 us (18%)
  matrix products  49.3 us (15%)
  blocking collectives  40.6 us (13%)
  between operations  14.1 us (4%)
  starting transfers between devices  11.4 us (4%)
  other arithmetic  10.3 us (3%)
    gather x8, local copies, waits for them, and re-layouts, on_device(): history[level][targets]  67.1 us
    all_to_all x2, blocking collectives, on_device(): lax.all_to_all(jnp.where(live_slots, history[level][targets], zero_value)...  40.6 us
    reshape x4, local copies, waits for them, and re-layouts, propagate(): picked = picked.reshape(row_tiles, per_row, tile_size, slice_width)  38.7 us
    all_to_all x2, waiting for transfers between devices, on_device(): lax.all_to_all(jnp.where(live_slots, history[level][targets], zero_value)...  28.1 us
    all_gather x4, waiting for transfers between devices, on_device(): lax.all_gather(blended, 'feat', axis=1, tiled=True)  27.7 us
    dot_general x4, matrix products, propagate(): jnp.einsum('rkab,rkbf->raf', values, picked, preferred_element_type=jnp.f...  27.1 us
    reshape x4, local copies, waits for them, and re-layouts, propagate(): flat_tiles = combined.reshape(tile_count, tile_size * slice_width)  14.1 us
    dot_general x4, matrix products, propagate(): jnp.dot(selector, flat_tiles, preferred_element_type=jnp.float32)  12.1 us
  transfers between devices with their start and end apart: 6, of which 6 were waited for; matrix products, arithmetic and copies ran while one was open for 1% of the time, Pallas kernels for 0%

commit v1 on v0

--- a/solution.py
+++ b/solution.py
@@ -7,6 +7,11 @@
 LAYERS = 4
 ALPHA = 0.1
 LAMBDA_DECAY = 0.5
+
+
+def gathered_along(x, name, dim):
+    shards = lax.all_gather(x, name)
+    return jnp.concatenate(shards, axis=dim)
 
 
 def propagate(own_rows, halo_rows, values, columns, tile_size):
@@ -63,9 +68,7 @@
         feat_index = lax.axis_index("feat")
         weight_cols = lax.dynamic_slice_in_dim(weight, feat_index * slice_width, slice_width, 1)
         product = jnp.dot(
-            lax.all_gather(blended, "feat", axis=1, tiled=True),
-            weight_cols,
-            preferred_element_type=jnp.float32,
+            gathered_along(blended, "feat", 1), weight_cols, preferred_element_type=jnp.float32
         )
         fresh = jnp.maximum(
             (1.0 - beta_layer) * blended.astype(jnp.float32) + beta_layer * product, 0.0

time: 319 us -> 307 us (0.962)
  matrix products: 49.3 us -> 43.1 us
  local copies, waits for them, and re-layouts: 135 us -> 131 us
    gather x8, local copies, waits for them, and re-layouts: 67.1 us -> 52.3 us  [on_device(): history[level][targets]]
    all_gather x0 -> x4, local copies, waits for them, and re-layouts: none -> 7.2 us  [gathered_along(): shards = lax.all_gather(x, name)]
    dot_general x4, matrix products: 9.64 us -> 3.43 us  [on_device(): jnp.dot(gathered_along(blended, 'feat', 1), weight_cols, preferred_elemen...]
where the time goes in v1:
time: 307 us; the launch traced here: 305 us
  local copies, waits for them, and re-layouts  131 us (43%)
  waiting for transfers between devices  56 us (18%)
  matrix products  43.1 us (14%)
  blocking collectives  40.4 us (13%)
  between operations  14.1 us (5%)
  starting transfers between devices  11.3 us (4%)
  other arithmetic  9.25 us (3%)
    gather x8, local copies, waits for them, and re-layouts, on_device(): history[level][targets]  52.3 us
    all_to_all x2, blocking collectives, on_device(): lax.all_to_all(jnp.where(live_slots, history[level][targets], zero_value)...  40.4 us
    reshape x4, local copies, waits for them, and re-layouts, propagate(): picked = picked.reshape(row_tiles, per_row, tile_size, slice_width)  38.7 us
    all_to_all x2, waiting for transfers between devices, on_device(): lax.all_to_all(jnp.where(live_slots, history[level][targets], zero_value)...  28.1 us
    all_gather x4, waiting for transfers between devices, gathered_along(): shards = lax.all_gather(x, name)  27.8 us
    dot_general x4, matrix products, propagate(): jnp.einsum('rkab,rkbf->raf', values, picked, preferred_element_type=jnp.f...  27.1 us
    reshape x4, local copies, waits for them, and re-layouts, propagate(): flat_tiles = combined.reshape(tile_count, tile_size * slice_width)  14.1 us
    dot_general x4, matrix products, propagate(): jnp.dot(selector, flat_tiles, preferred_element_type=jnp.float32)  12.1 us
  transfers between devices with their start and end apart: 6, of which 6 were waited for; matrix products, arithmetic and copies ran while one was open for 1% of the time, Pallas kernels for 0%

profile of v1, /device:TPU:0, one launch (start us, length us, event | category | flops | bytes accessed | tf_op | source)
XLA Modules:
  0.0 305.0 jit_solution(770989398882846970)
XLA Ops:
  7.2 2.8 fusion.42
  10.5 12.1 %gather_fusion = bf16[4096,64]{1,0:T(8,128)(2,1)S(1)} fusion(bf16[4096,64]{1,0:T(8,128)(2,1)S(1)} %bitcast.141, s32[4096]{0:T(1024)S(1)} %broadcast_clamp_fusion), kind=kCustom, calls=%fused_computation | custom fusion | bytes 1064960 | tf_op jit(solution)/shard_map/gather | solution.py:47
  22.7 1.1 copy.53
  23.8 1.5 copy.89
  25.3 12.1 %gather_fusion.1 = bf16[4096,64]{1,0:T(8,128)(2,1)S(1)} fusion(bf16[4096,64]{1,0:T(8,128)(2,1)S(1)} %bitcast.143, s32[4096]{0:T(1024)S(1)} %broadcast_clamp_fusion), kind=kCustom, calls=%fused_computation.1 | custom fusion | bytes 1064960 | tf_op jit(solution)/shard_map/gather | solution.py:47
  37.5 1.1 copy.60
  38.6 1.5 copy.90
  40.1 12.1 %gather_fusion.2 = bf16[4096,64]{1,0:T(8,128)(2,1)S(1)} fusion(bf16[4096,64]{1,0:T(8,128)(2,1)S(1)} %bitcast.144, s32[4096]{0:T(1024)S(1)} %broadcast_clamp_fusion), kind=kCustom, calls=%fused_computation.2 | custom fusion | bytes 1064960 | tf_op jit(solution)/shard_map/gather | solution.py:47
  52.3 1.1 copy.67
  53.4 1.5 copy.91
  54.9 12.1 %gather_fusion.3 = bf16[4096,64]{1,0:T(8,128)(2,1)S(1)} fusion(bf16[4096,64]{1,0:T(8,128)(2,1)S(1)} %bitcast.142, s32[4096]{0:T(1024)S(1)} %broadcast_clamp_fusion), kind=kCustom, calls=%fused_computation.3 | custom fusion | bytes 1064960 | tf_op jit(solution)/shard_map/gather | solution.py:47
  67.5 2.5 broadcast_select_fusion
  70.0 7.3 %all-to-all-start = ((bf16[8,512,64]{1,2,0:T(8,128)(2,1)}), bf16[8,512,64]{1,2,0:T(8,128)(2,1)S(1)}, u32[]{:S(2)}, u32[]{:S(2)}) async-start(bf16[8,512,64]{1,2,0:T(8,128)(2,1)} %get-tuple-element.13), calls=%async_computation | async-start | bytes 1048576 | tf_op jit(solution)/shard_map/all_to_all | solution.py:46
  78.1 13.7 %all-to-all-done = bf16[8,512,64]{1,2,0:T(8,128)(2,1)S(1)} async-done(((bf16[8,512,64]{1,2,0:T(8,128)(2,1)}), bf16[8,512,64]{1,2,0:T(8,128)(2,1)S(1)}, u32[]{:S(2)}, u32[]{:S(2)}) %all-to-all-start) | async-done | bytes 524320 | tf_op jit(solution)/shard_map/all_to_all | solution.py:46
  91.9 1.8 copy.55
  93.7 3.3 %reshape.138 = bf16[64,8192]{1,0:T(8,128)(2,1)S(1)} reshape(bf16[8192,64]{1,0:T(8,128)(2,1)} %copy.55) | data formatting | bytes 2097152 | tf_op jit(solution)/shard_map/reshape | solution.py:21
  97.0 2.7 convolution_convert_fusion.3
  99.7 9.7 %reshape.139 = bf16[32,6,128,64]{3,2,1,0:T(8,128)(2,1)} reshape(bf16[192,8192]{1,0:T(8,128)(2,1)} %convolution_convert_fusion.3) | data formatting | bytes 6291456 | tf_op jit(solution)/shard_map/reshape | solution.py:27
  109.4 6.8 %fusion.14 = f32[32,8,8,128]{3,2,1,0:T(8,128)S(1)} fusion(bf16[32,6,128,64]{3,2,1,0:T(8,128)(2,1)} %reshape.139, bf16[32,6,128,128]{3,2,1,0:T(8,128)(2,1)} %param.12), kind=kOutput, calls=%fused_computation.36 | convolution fusion | flops 402915328 | bytes 10485760 | tf_op jit(solution)/shard_map/rkab,rkbf->raf/dot_general | solution.py:28
  117.1 3.7 %all-to-all-start.1 = ((bf16[8,512,64]{1,2,0:T(8,128)(2,1)}), bf16[8,512,64]{1,2,0:T(8,128)(2,1)S(1)}, u32[]{:S(2)}, u32[]{:S(2)}) async-start(bf16[8,512,64]{1,2,0:T(8,128)(2,1)} %get-tuple-element.11), calls=%async_computation.1 | async-start | bytes 1048576 | tf_op jit(solution)/shard_map/all_to_all | solution.py:46
  121.1 14.4 %all-to-all-done.1 = bf16[8,512,64]{1,2,0:T(8,128)(2,1)S(1)} async-done(((bf16[8,512,64]{1,2,0:T(8,128)(2,1)}), bf16[8,512,64]{1,2,0:T(8,128)(2,1)S(1)}, u32[]{:S(2)}, u32[]{:S(2)}) %all-to-all-start.1) | async-done | bytes 524320 | tf_op jit(solution)/shard_map/all_to_all | solution.py:46
  136.3 2.6 all-gather.9.cloned.1.call-done
  138.9 1.8 copy.116
  141.9 1.8 copy.62
  143.6 3.3 %reshape.143 = bf16[64,8192]{1,0:T(8,128)(2,1)S(1)} reshape(bf16[8192,64]{1,0:T(8,128)(2,1)} %copy.62) | data formatting | bytes 2097152 | tf_op jit(solution)/shard_map/reshape | solution.py:21
  146.9 2.7 convolution_convert_fusion.2
  149.7 9.7 %reshape.144 = bf16[32,6,128,64]{3,2,1,0:T(8,128)(2,1)} reshape(bf16[192,8192]{1,0:T(8,128)(2,1)} %convolution_convert_fusion.2) | data formatting | bytes 6291456 | tf_op jit(solution)/shard_map/reshape | solution.py:27
  159.3 6.8 %fusion.16 = f32[32,8,8,128]{3,2,1,0:T(8,128)S(1)} fusion(bf16[32,6,128,64]{3,2,1,0:T(8,128)(2,1)} %reshape.144, bf16[32,6,128,128]{3,2,1,0:T(8,128)(2,1)} %param.12), kind=kOutput, calls=%fused_computation.38 | convolution fusion | flops 402915328 | bytes 10485760 | tf_op jit(solution)/shard_map/rkab,rkbf->raf/dot_general | solution.py:28
  167.1 20.2 %all_to_all.20 = bf16[8,512,64]{1,2,0:T(8,128)(2,1)S(1)} all-to-all(bf16[8,512,64]{1,2,0:T(8,128)(2,1)S(1)} %get-tuple-element.12), channel_id=1, replica_groups=mesh['feat'=4,'dom'=8] {'dom'}, dimensions={0} | all-to-all | bytes 1048576 | tf_op jit(solution)/shard_map/all_to_all | solution.py:46
  188.2 1.6 all-gather.11.cloned.1.call-done
  189.8 1.8 copy.115
  192.7 1.8 copy.69
  194.5 3.3 %reshape.148 = bf16[64,8192]{1,0:T(8,128)(2,1)S(1)} reshape(bf16[8192,64]{1,0:T(8,128)(2,1)} %copy.69) | data formatting | bytes 2097152 | tf_op jit(solution)/shard_map/reshape | solution.py:21
  197.8 2.7 convolution_convert_fusion.1
  200.5 9.7 %reshape.149 = bf16[32,6,128,64]{3,2,1,0:T(8,128)(2,1)} reshape(bf16[192,8192]{1,0:T(8,128)(2,1)} %convolution_convert_fusion.1) | data formatting | bytes 6291456 | tf_op jit(solution)/shard_map/reshape | solution.py:27
  210.2 6.8 %fusion.18 = f32[32,8,8,128]{3,2,1,0:T(8,128)S(1)} fusion(bf16[32,6,128,64]{3,2,1,0:T(8,128)(2,1)} %reshape.149, bf16[32,6,128,128]{3,2,1,0:T(8,128)(2,1)} %param.12), kind=kOutput, calls=%fused_computation.40 | convolution fusion | flops 402915328 | bytes 10485760 | tf_op jit(solution)/shard_map/rkab,rkbf->raf/dot_general | solution.py:28
  218.0 20.2 %all_to_all.21 = bf16[8,512,64]{1,2,0:T(8,128)(2,1)S(1)} all-to-all(bf16[8,512,64]{1,2,0:T(8,128)(2,1)S(1)} %copy-done.6), channel_id=1, replica_groups=mesh['feat'=4,'dom'=8] {'dom'}, dimensions={0} | all-to-all | bytes 1048576 | tf_op jit(solution)/shard_map/all_to_all | solution.py:46
  238.2 2.4 all-gather.13.cloned.1.call-done
  240.7 1.8 copy.114
  244.2 2.7 copy.76
  246.9 4.2 %reshape.153 = bf16[64,8192]{1,0:T(8,128)(2,1)} reshape(bf16[8192,64]{1,0:T(8,128)(2,1)} %copy.76) | data formatting | bytes 2097152 | tf_op jit(solution)/shard_map/reshape | solution.py:21
  251.1 3.9 %convolution_convert_fusion = bf16[192,8192]{1,0:T(8,128)(2,1)} fusion(bf16[64,8192]{1,0:T(8,128)(2,1)} %reshape.153, s32[192]{0:T(256)S(1)} %eq.8), kind=kOutput, calls=%fused_computation.4 | convolution fusion | flops 202911744 | bytes 4195072 | tf_op jit(solution)/shard_map/dot_general | solution.py:26
  255.0 9.7 %reshape.154 = bf16[32,6,128,64]{3,2,1,0:T(8,128)(2,1)} reshape(bf16[192,8192]{1,0:T(8,128)(2,1)} %convolution_convert_fusion) | data formatting | bytes 6291456 | tf_op jit(solution)/shard_map/reshape | solution.py:27
  264.7 6.8 %fusion.20 = f32[32,8,8,128]{3,2,1,0:T(8,128)S(1)} fusion(bf16[32,6,128,64]{3,2,1,0:T(8,128)(2,1)} %reshape.154, bf16[32,6,128,128]{3,2,1,0:T(8,128)(2,1)} %param.12), kind=kOutput, calls=%fused_computation.42 | convolution fusion | flops 402915328 | bytes 10485760 | tf_op jit(solution)/shard_map/rkab,rkbf->raf/dot_general | solution.py:28
  272.4 1.6 pad_maximum_fusion
  274.0 21.1 %all-gather.15.cloned.1.call-done = bf16[16384,64]{0,1:T(8,128)(2,1)} async-done(((bf16[4096,64]{0,1:T(8,128)(2,1)}), bf16[16384,64]{0,1:T(8,128)(2,1)}) %all-gather.15.cloned.1.call-update) | async-done | bytes 2097168 | tf_op jit(solution)/shard_map/all_gather | solution.py:13
  295.1 1.8 copy.113
  297.0 1.5 fusion.8
  (61 shorter events, 11.6 us)
Async XLA Ops:
  7.2 70.4 %copy-start = (bf16[4096,128]{1,0:T(8,128)(2,1)S(1)}, bf16[4096,128]{1,0:T(8,128)(2,1)}, u32[]{:S(2)}) copy-start(bf16[4096,128]{1,0:T(8,128)(2,1)} %param.8) | copy-start | bytes 3145732
  7.2 3.3 %copy-start.11 = (s32[1,8,512]{2,1,0:T(8,128)S(1)}, s32[1,8,512]{2,1,0:T(8,128)}, u32[]{:S(2)}) copy-start(s32[1,8,512]{2,1,0:T(8,128)} %param.14) | copy-start | bytes 49156
  54.9 12.5 %copy-start.13 = (s32[1,8]{1,0:T(1,128)S(1)}, s32[1,8]{1,0:T(1,128)}, u32[]{:S(2)}) copy-start(s32[1,8]{1,0:T(1,128)} %param.15) | copy-start | bytes 100
  67.5 9.9 %copy-start.12 = (s32[32,6]{0,1:T(8,128)S(1)}, s32[32,6]{0,1:T(8,128)}, u32[]{:S(2)}) copy-start(s32[32,6]{0,1:T(8,128)} %param.13) | copy-start | bytes 2308
  67.5 10.1 %copy-start.10 = (bf16[128,64]{0,1:T(8,128)(2,1)S(1)}, bf16[128,64]{0,1:T(8,128)(2,1)}, u32[]{:S(2)}) copy-start(bf16[128,64]{0,1:T(8,128)(2,1)} %param.9) | copy-start | bytes 49156
  70.0 21.8 %all-to-all-start = ((bf16[8,512,64]{1,2,0:T(8,128)(2,1)}), bf16[8,512,64]{1,2,0:T(8,128)(2,1)S(1)}, u32[]{:S(2)}, u32[]{:S(2)}) async-start(bf16[8,512,64]{1,2,0:T(8,128)(2,1)} %get-tuple-element.13), calls=%async_computation | async-start | bytes 1048576 | tf_op jit(solution)/shard_map/all_to_all | solution.py:46
  77.3 61.6 %all-gather.9.cloned.1.call-start = ((), (), s32[]{:S(2)}) async-start(), calls=%async_computation.4 | async-start | bytes 2621440 | tf_op jit(solution)/shard_map/all_gather | solution.py:13
  116.2 4.9 %copy-start.9 = (bf16[4,256,256]{2,1,0:T(8,128)(2,1)S(1)}, bf16[4,256,256]{2,1,0:T(8,128)(2,1)}, u32[]{:S(2)}) copy-start(bf16[4,256,256]{2,1,0:T(8,128)(2,1)} %param.10) | copy-start | bytes 1572868
  117.1 18.3 %all-to-all-start.1 = ((bf16[8,512,64]{1,2,0:T(8,128)(2,1)}), bf16[8,512,64]{1,2,0:T(8,128)(2,1)S(1)}, u32[]{:S(2)}, u32[]{:S(2)}) async-start(bf16[8,512,64]{1,2,0:T(8,128)(2,1)} %get-tuple-element.11), calls=%async_computation.1 | async-start | bytes 1048576 | tf_op jit(solution)/shard_map/all_to_all | solution.py:46
  120.8 69.0 %all-gather.11.cloned.1.call-start = ((), (), s32[]{:S(2)}) async-start(), calls=%async_computation.5 | async-start | bytes 2621440 | tf_op jit(solution)/shard_map/all_gather | solution.py:13
  138.9 1.8 copy-start.2
  140.7 1.0 copy-start.7
  167.1 73.6 %all-gather.13.cloned.1.call-start = ((), (), s32[]{:S(2)}) async-start(), calls=%async_computation.6 | async-start | bytes 2621440 | tf_op jit(solution)/shard_map/all_gather | solution.py:13
  189.8 1.8 copy-start.5
  191.6 1.0 copy-start.8
  217.0 1.0 copy-start.6
  217.9 77.2 %all-gather.15.cloned.1.call-start = ((), (), s32[]{:S(2)}) async-start(), calls=%async_computation.7 | async-start | bytes 2621440 | tf_op jit(solution)/shard_map/all_gather | solution.py:13
  240.7 1.8 copy-start.3
  295.1 1.9 copy-start.4
  295.1 3.3 %copy-start.1 = (bf16[4096,128]{1,0:T(8,128)(2,1)S(1)}, bf16[4096,128]{1,0:T(8,128)(2,1)}, u32[]{:S(2)}) copy-start(bf16[4096,128]{1,0:T(8,128)(2,1)} %param.8) | copy-start | bytes 3145732
Sparse Core Ops, SparseCore 0:
  117.3 21.6 all-gather.8
  167.2 22.5 all-gather.10
  218.1 22.5 all-gather.12
  272.5 22.5 all-gather.14
